TPU v7x, 256 devices: a whole 4x4x8 slice. The times are simulated.
256 devices in a mesh: dp: 32 (over x_hi, z, core), tensor: 8 (over y, x_lo).
Axes of the slice: x: 4 (x_hi: 2, x_lo: 2; x = x_hi * 2 + x_lo), y: 4, z: 8, core: 2. Of those that a mesh axis runs over, the one named last changes fastest.
Arguments:
- grad_hidden: bfloat16 [4096, 14336], P('dp', 'tensor'), may hold values from -18 to 18
- gate: bfloat16 [4096, 14336], P('dp', 'tensor'), may hold values from -6 to 6
Outputs:
- factor: float32 [14336, 14336], P('tensor', 'dp')
All inputs are finite; a program needn't handle non-finite values.
Results may differ from a plain program's by a relative error of at most 0.0065.
Values may be sent and summed in bfloat16 or wider, within the bound.
A program may use at most 128 MiB of HBM per device.

v0:
```python
import jax
import jax.numpy as jnp
from jax import lax
from jax.sharding import PartitionSpec as P

FF = 14336


def broadcast(block, axis, owner):
    block = jnp.where(lax.axis_index(axis) == owner, block, jnp.zeros_like(block))
    return lax.psum(block, axis)


def shards(grad_hidden, gate):
    up_grad = (grad_hidden.astype(jnp.float32) * jax.nn.silu(gate.astype(jnp.float32))).astype(
        jnp.bfloat16
    )
    tensor_count = lax.axis_size("tensor")
    data_count = lax.axis_size("dp")
    col_width = FF // data_count
    ratio = data_count // tensor_count
    data_index = lax.axis_index("dp")
    owner = data_index // ratio
    offset = data_index % ratio * col_width
    contract = (((0,), (0,)), ((), ()))
    total_tokens = up_grad.shape[0] * data_count
    rows_all = lax.all_gather(up_grad, "dp", axis=0, tiled=True)
    panel = lax.dynamic_slice_in_dim(rows_all, offset, col_width, 1)
    cols_all = broadcast(panel, "tensor", owner)
    summed = lax.dot_general(rows_all, cols_all, contract, preferred_element_type=jnp.float32)
    return summed / total_tokens


def solution(mesh):
    return jax.shard_map(
        shards,
        mesh=mesh,
        in_specs=(P("dp", "tensor"), P("dp", "tensor")),
        out_specs=P("tensor", "dp"),
        check_vma=False,
    )
```

profile of v0, /device:TPU:1, one launch (start us, length us, event | category | flops | bytes accessed | tf_op | source)
XLA Modules:
  0.0 352.8 jit_solution(12489471338623991828)
XLA Ops:
  6.5 0.0 all-gather.2.cloned.1.call-start
  6.5 2.2 fusion.4
  8.7 0.0 all-gather.2.cloned.1.call-update
  8.8 0.0 all-reduce.2.cloned.1.call-start
  8.8 132.4 %all-gather.2.cloned.1.call-done = bf16[4096,1792]{1,0:T(8,128)(2,1)} async-done(((bf16[128,1792]{1,0:T(8,128)(2,1)}), bf16[4096,1792]{1,0:T(8,128)(2,1)}) %all-gather.2.cloned.1.call-update) | async-done | bytes 14680080 | tf_op jit(solution)/shard_map/all_gather | solution.py:27
  141.3 7.3 %dynamic-slice_select_fusion = bf16[4096,448]{1,0:T(8,128)(2,1)} fusion(bf16[4096,1792]{1,0:T(8,128)(2,1)} %all-gather.2.cloned.1.call-done, s32[]{:T(128)S(6)} %select_n.25, pred[]{:T(512)S(6)} %eq.5), kind=kLoop, calls=%fused_computation | loop fusion | flops 1835008 | bytes 7340037 | tf_op jit(solution)/shard_map/jit(_where)/select_n | solution.py:10
  148.6 0.0 all-reduce.2.cloned.1.call-update
  148.6 184.0 %all-reduce.2.cloned.1.call-done = bf16[4096,448]{1,0:T(8,128)(2,1)} async-done(((bf16[4096,448]{1,0:T(8,128)(2,1)}), bf16[4096,448]{1,0:T(8,128)(2,1)}) %all-reduce.2.cloned.1.call-update) | async-done | bytes 3670032 | tf_op jit(solution)/shard_map/psum | solution.py:11
  332.6 13.4 %convolution_multiply_fusion = f32[1792,448]{0,1:T(8,128)} fusion(bf16[4096,1792]{1,0:T(8,128)(2,1)} %all-gather.2.cloned.1.call-done, bf16[4096,448]{1,0:T(8,128)(2,1)} %all-reduce.2.cloned.1.call-done), kind=kOutput, calls=%fused_computation.1 | convolution fusion | flops 6577471488 | bytes 21561344 | tf_op jit(solution)/shard_map/dot_general | solution.py:30
Async XLA Ops:
  6.5 134.7 %all-gather.2.cloned.1.call-start = ((), (), s32[]{:S(2)}) async-start(), calls=%async_computation | async-start | bytes 15138816 | tf_op jit(solution)/shard_map/all_gather | solution.py:27
  8.8 323.8 %all-reduce.2.cloned.1.call-start = ((), (), s32[]{:S(2)}) async-start(), calls=%async_computation.1 | async-start | bytes 8388608 | tf_op jit(solution)/shard_map/psum | solution.py:11
Sparse Core Ops, SparseCore 0:
  10.1 131.1 all-gather.1
  148.7 183.7 all-reduce.1
where the time goes:
time: 353 us
  waiting for transfers between devices  316 us (90%)
  matrix products  13.4 us (4%)
  between operations  13.4 us (4%)
  other arithmetic  9.53 us (3%)
    psum x1, waiting for transfers between devices, broadcast(): return lax.psum(block, axis)  184 us
    all_gather x1, waiting for transfers between devices, shards(): rows_all = lax.all_gather(up_grad, 'dp', axis=0, tiled=True)  132 us
    dot_general x1, matrix products, shards(): lax.dot_general(rows_all, cols_all, contract, preferred_element_type=jnp....  13.4 us
    select_n x1, other arithmetic, broadcast(): jnp.where(lax.axis_index(axis) == owner, block, jnp.zeros_like(block))  7.33 us
  transfers between devices with their start and end apart: 2, of which 2 were waited for; matrix products, arithmetic and copies ran while one was open for 0% of the time, Pallas kernels for 0%

commit v1 on v0

--- a/solution.py
+++ b/solution.py
@@ -24,7 +24,9 @@
     offset = data_index % ratio * col_width
     contract = (((0,), (0,)), ((), ()))
     total_tokens = up_grad.shape[0] * data_count
-    rows_all = lax.all_gather(up_grad, "dp", axis=0, tiled=True)
+    rows_all = jnp.concatenate(
+        lax.all_to_all(jnp.stack([up_grad] * lax.axis_size("dp")), "dp", 0, 0), axis=0
+    )
     panel = lax.dynamic_slice_in_dim(rows_all, offset, col_width, 1)
     cols_all = broadcast(panel, "tensor", owner)
     summed = lax.dot_general(rows_all, cols_all, contract, preferred_element_type=jnp.float32)

time: 353 us -> 567 us (1.61)
  waiting for transfers between devices: 316 us -> 512 us
  starting transfers between devices: 0.04 us -> 12.7 us
  local copies, waits for them, and re-layouts: 0 us -> 6.85 us
    all_to_all x0 -> x1, waiting for transfers between devices: none -> 318 us  [shards(): lax.all_to_all(jnp.stack([up_grad] * lax.axis_size('dp')), 'dp', 0, 0)]
    all_gather x1 -> x0, waiting for transfers between devices: 132 us -> none  [shards(): rows_all = lax.all_gather(up_grad, 'dp', axis=0, tiled=True)]
    all_to_all x0 -> x1, starting transfers between devices: none -> 12.6 us  [shards(): lax.all_to_all(jnp.stack([up_grad] * lax.axis_size('dp')), 'dp', 0, 0)]
    psum x1, waiting for transfers between devices: 184 us -> 193 us  [broadcast(): return lax.psum(block, axis)]
    another operation x0 -> x1, local copies, waits for them, and re-layouts: none -> 6.85 us  [shards(): jnp.stack([up_grad] * lax.axis_size('dp'))]
where the time goes in v1:
time: 567 us
  waiting for transfers between devices  512 us (90%)
  matrix products  13.4 us (2%)
  between operations  13.4 us (2%)
  starting transfers between devices  12.7 us (2%)
  other arithmetic  8.77 us (2%)
  local copies, waits for them, and re-layouts  6.85 us (1%)
    all_to_all x1, waiting for transfers between devices, shards(): lax.all_to_all(jnp.stack([up_grad] * lax.axis_size('dp')), 'dp', 0, 0)  318 us
    psum x1, waiting for transfers between devices, broadcast(): return lax.psum(block, axis)  193 us
    dot_general x1, matrix products, shards(): lax.dot_general(rows_all, cols_all, contract, preferred_element_type=jnp....  13.4 us
    all_to_all x1, starting transfers between devices, shards(): lax.all_to_all(jnp.stack([up_grad] * lax.axis_size('dp')), 'dp', 0, 0)  12.6 us
  transfers between devices with their start and end apart: 2, of which 2 were waited for; matrix products, arithmetic and copies ran while one was open for 0% of the time, Pallas kernels for 0%

profile of v1, /device:TPU:1, one launch (start us, length us, event | category | flops | bytes accessed | tf_op | source)
XLA Modules:
  0.0 567.1 jit_solution(14314838638314270907)
XLA Ops:
  6.5 1.4 fusion.4
  8.0 6.8 %stack.2 = bf16[32,128,1792]{2,1,0:T(8,128)(2,1)} broadcast(bf16[128,1792]{1,0:T(8,128)(2,1)S(1)} %fusion.4), dimensions={1,2} | broadcast | bytes 15138816 | tf_op jit(solution)/shard_map/stack | solution.py:28
  14.8 12.6 %all-to-all-start = ((bf16[32,128,1792]{2,1,0:T(8,128)(2,1)}), bf16[32,128,1792]{2,1,0:T(8,128)(2,1)}, u32[]{:S(2)}, u32[]{:S(2)}) async-start(bf16[32,128,1792]{2,1,0:T(8,128)(2,1)} %stack.2), calls=%async_computation | async-start | bytes 29360128 | tf_op jit(solution)/shard_map/all_to_all | solution.py:28
  27.5 0.0 all-reduce.2.cloned.1.call-start
  27.5 318.5 %all-to-all-done = bf16[32,128,1792]{2,1,0:T(8,128)(2,1)} async-done(((bf16[32,128,1792]{2,1,0:T(8,128)(2,1)}), bf16[32,128,1792]{2,1,0:T(8,128)(2,1)}, u32[]{:S(2)}, u32[]{:S(2)}) %all-to-all-start) | async-done | bytes 14680096 | tf_op jit(solution)/shard_map/all_to_all | solution.py:28
  346.0 7.3 %dynamic-slice_select_fusion = bf16[4096,448]{1,0:T(8,128)(2,1)} fusion(bf16[4096,1792]{1,0:T(8,128)(2,1)} %bitcast, s32[]{:T(128)S(6)} %select_n.25, pred[]{:T(512)S(6)} %eq.5), kind=kLoop, calls=%fused_computation | loop fusion | flops 1835008 | bytes 7340037 | tf_op jit(solution)/shard_map/jit(_where)/select_n | solution.py:10
  353.4 0.0 all-reduce.2.cloned.1.call-update
  353.4 193.4 %all-reduce.2.cloned.1.call-done = bf16[4096,448]{1,0:T(8,128)(2,1)} async-done(((bf16[4096,448]{1,0:T(8,128)(2,1)}), bf16[4096,448]{1,0:T(8,128)(2,1)}) %all-reduce.2.cloned.1.call-update) | async-done | bytes 3670032 | tf_op jit(solution)/shard_map/psum | solution.py:11
  546.8 13.4 %convolution_multiply_fusion = f32[1792,448]{0,1:T(8,128)} fusion(bf16[4096,1792]{1,0:T(8,128)(2,1)} %bitcast, bf16[4096,448]{1,0:T(8,128)(2,1)} %all-reduce.2.cloned.1.call-done), kind=kOutput, calls=%fused_computation.1 | convolution fusion | flops 6577471488 | bytes 21561344 | tf_op jit(solution)/shard_map/dot_general | solution.py:32
Async XLA Ops:
  14.8 331.2 %all-to-all-start = ((bf16[32,128,1792]{2,1,0:T(8,128)(2,1)}), bf16[32,128,1792]{2,1,0:T(8,128)(2,1)}, u32[]{:S(2)}, u32[]{:S(2)}) async-start(bf16[32,128,1792]{2,1,0:T(8,128)(2,1)} %stack.2), calls=%async_computation | async-start | bytes 29360128 | tf_op jit(solution)/shard_map/all_to_all | solution.py:28
  27.5 519.4 %all-reduce.2.cloned.1.call-start = ((), (), s32[]{:S(2)}) async-start(), calls=%async_computation.1 | async-start | bytes 8388608 | tf_op jit(solution)/shard_map/psum | solution.py:11
Sparse Core Ops, SparseCore 0:
  353.5 193.2 all-reduce.1

commit v2 on v0

--- a/solution.py
+++ b/solution.py
@@ -8,7 +8,7 @@
 
 def broadcast(block, axis, owner):
     block = jnp.where(lax.axis_index(axis) == owner, block, jnp.zeros_like(block))
-    return lax.psum(block, axis)
+    return jnp.sum(lax.all_gather(block, axis), axis=0)
 
 
 def shards(grad_hidden, gate):

time: 353 us -> 822 us (2.33)
  waiting for transfers between devices: 316 us -> 772 us
  other arithmetic: 9.53 us -> 23.6 us
    all_gather x0 -> x1, waiting for transfers between devices: none -> 639 us  [broadcast(): return jnp.sum(lax.all_gather(block, axis), axis=0)]
    psum x1 -> x0, waiting for transfers between devices: 184 us -> none  [broadcast(): return lax.psum(block, axis)]
    reduce_sum x0 -> x1, other arithmetic: none -> 14.1 us  [broadcast(): return jnp.sum(lax.all_gather(block, axis), axis=0)]
where the time goes in v2:
time: 822 us
  waiting for transfers between devices  772 us (94%)
  other arithmetic  23.6 us (3%)
  matrix products  13.4 us (2%)
  between operations  13.4 us (2%)
    all_gather x1, waiting for transfers between devices, broadcast(): return jnp.sum(lax.all_gather(block, axis), axis=0)  639 us
    all_gather x1, waiting for transfers between devices, shards(): rows_all = lax.all_gather(up_grad, 'dp', axis=0, tiled=True)  132 us
  transfers between devices with their start and end apart: 2, of which 2 were waited for; matrix products, arithmetic and copies ran while one was open for 0% of the time, Pallas kernels for 0%

profile of v2, /device:TPU:1, one launch (start us, length us, event | category | flops | bytes accessed | tf_op | source)
XLA Modules:
  0.0 822.0 jit_solution(3667939706331458940)
XLA Ops:
  6.5 0.0 all-gather.4.cloned.1.call-start
  6.5 2.2 fusion.4
  8.7 0.0 all-gather.4.cloned.1.call-update
  8.8 0.0 all-gather.6.cloned.1.call-start
  8.8 132.4 %all-gather.4.cloned.1.call-done = bf16[4096,1792]{1,0:T(8,128)(2,1)} async-done(((bf16[128,1792]{1,0:T(8,128)(2,1)}), bf16[4096,1792]{1,0:T(8,128)(2,1)}) %all-gather.4.cloned.1.call-update) | async-done | bytes 14680080 | tf_op jit(solution)/shard_map/all_gather | solution.py:27
  141.3 7.3 dynamic-slice_select_fusion
  148.5 0.0 all-gather.6.cloned.1.call-update
  148.5 639.1 %all-gather.6.cloned.1.call-done = bf16[32768,448]{1,0:T(8,128)(2,1)} async-done(((bf16[4096,448]{1,0:T(8,128)(2,1)}), bf16[32768,448]{1,0:T(8,128)(2,1)}) %all-gather.6.cloned.1.call-update) | async-done | bytes 29360144 | tf_op jit(solution)/shard_map/all_gather | solution.py:11
  787.6 14.1 %reduce_sum.12 = bf16[4096,448]{1,0:T(8,128)(2,1)} reduce(bf16[8,4096,448]{2,1,0:T(8,128)(2,1)} %bitcast.3, bf16[]{:T(256)} %constant.48.clone.1), dimensions={0}, to_apply=%region_0.1 | reduce | flops 12845056 | bytes 33030146 | tf_op jit(solution)/shard_map/reduce_sum | solution.py:11
  801.7 13.4 %convolution_multiply_fusion = f32[1792,448]{0,1:T(8,128)} fusion(bf16[4096,1792]{1,0:T(8,128)(2,1)} %all-gather.4.cloned.1.call-done, bf16[4096,448]{1,0:T(8,128)(2,1)} %reduce_sum.12), kind=kOutput, calls=%fused_computation.1 | convolution fusion | flops 6577471488 | bytes 21561344 | tf_op jit(solution)/shard_map/dot_general | solution.py:30
Async XLA Ops:
  6.5 134.7 %all-gather.4.cloned.1.call-start = ((), (), s32[]{:S(2)}) async-start(), calls=%async_computation | async-start | bytes 15138816 | tf_op jit(solution)/shard_map/all_gather | solution.py:27
  8.8 778.8 %all-gather.6.cloned.1.call-start = ((), (), s32[]{:S(2)}) async-start(), calls=%async_computation.1 | async-start | bytes 37748736 | tf_op jit(solution)/shard_map/all_gather | solution.py:11
Sparse Core Ops, SparseCore 0:
  10.1 131.1 all-gather.3
  148.7 638.8 all-gather.5
